TPU v7x, 128 devices: a whole 4x4x4 slice. The times are simulated.
128 devices in a mesh: row: 4 (over z), col: 32 (over x, y, core).
Axes of the slice: x: 4, y: 4, z: 4, core: 2. Of those that a mesh axis runs over, the one named last changes fastest.
Arguments:
- neighbor: int32 [32, 3072, 3072], P(None, 'col', 'row'), may hold values from 0 to 1, as said below
- true_coords: float32 [32, 3, 3072], P(None, None, ('row', 'col')), as said below
- pred_coords: float32 [32, 3, 3072], P(None, None, ('row', 'col')), as said below
- residue_mask: int32 [32, 3072], P(None, ('row', 'col')), may hold values from 0 to 1, as said below
- single: bfloat16 [32, 3072, 384], P(None, ('row', 'col'))
- ln_gain: float32 [384], replicated, may hold values from 0.1 to 1.9
- w_hidden: bfloat16 [384, 128], replicated, may hold values from -0.3125 to 0.3125
- b_hidden: float32 [128], replicated, may hold values from -3 to 3
- w_mid: bfloat16 [128, 128], replicated, may hold values from -0.5 to 0.5
- b_mid: float32 [128], replicated, may hold values from -3 to 3
- w_logits: bfloat16 [128, 50], replicated, may hold values from -1.5 to 1.5
- b_logits: float32 [50], replicated, may hold values from -4 to 4
Outputs:
- lddt_score: float32 [32, 3072], P(None, ('row', 'col'))
- residue_loss: float32 [32, 3072], P(None, ('row', 'col'))
- total_loss: float32 [], replicated
Inputs may be any that keep to these rules, and one draw needn't show every extreme that they name: `neighbor`: 0 or 1; 0 where j == i; 1 wherever 0 < |i - j| <= 8. `residue_mask`: per structure, 1 on a leading run of 1536 or more residues and 0 after it. `true_coords`: positions in angstroms. `pred_coords`: positions in angstroms.
All inputs are finite; a program needn't handle non-finite values.
Results may differ from a plain program's by a relative error of at most 0.00098.
Values sent between devices are 32-bit elements; how exact they have to be, the bound alone decides.
A program may use at most 64 MiB of HBM per device.

v0:
```python
import jax
import jax.numpy as jnp
from jax import lax
from jax.sharding import Mesh
from jax.sharding import PartitionSpec as P

L = 3072
COL = ("col_0", "col_1", "col_2")
ROW_COL = ("row", "col_0", "col_1", "col_2")
THRESHOLDS = (0.5, 1.0, 2.0, 4.0)


def in_order(parts, dim):
    parts = jnp.moveaxis(parts, 0, dim)
    lengths = parts.shape
    return parts.reshape(*lengths[:dim], lengths[dim] * lengths[dim + 1], *lengths[dim + 2 :])


def sent_to_all(shard, axis):
    copies = jnp.broadcast_to(shard, (lax.axis_size(axis), *shard.shape))
    return lax.all_to_all(copies, axis, split_axis=0, concat_axis=0, tiled=True)


def gather_directly(shard, axis, dim):
    return in_order(sent_to_all(shard, axis), dim)


def from_root(shard, axis, root):
    return lax.dynamic_index_in_dim(lax.all_gather(shard, axis), root, 0, keepdims=False)


def split_up(shard, dim, size):
    before, after = (shard.shape[:dim], shard.shape[dim + 1 :])
    return jnp.moveaxis(shard.reshape(*before, size, -1, *after), dim, 0)


def summed_on_arrival(shard, axis, dim):
    size = lax.axis_size(axis)
    parts = lax.all_to_all(split_up(shard, dim, size), axis, 0, 0, tiled=True)
    return jnp.sum(parts, axis=0)


def sent_together(arrays, axis, dim, along):
    ends, at = ([], 0)
    for a in arrays[:-1]:
        at += a.shape[along]
        ends.append(at)
    both = jnp.concatenate(arrays, axis=along)
    return tuple(jnp.split(summed_on_arrival(both, axis, dim), ends, axis=along))


def over_axes(shard, axes):
    for axis in axes:
        shard = lax.psum(shard, axis)
    return shard


def tile_dist(rows_block, cols_block):
    total = (cols_block[:, 0, :, None] - rows_block[:, 0, None, :]) ** 2
    total = total + (cols_block[:, 1, :, None] - rows_block[:, 1, None, :]) ** 2
    total = total + (cols_block[:, 2, :, None] - rows_block[:, 2, None, :]) ** 2
    return jnp.sqrt(total + 1e-10)


def head_loss(lddt_value, single, ln_gain, w_hidden, b_hidden, w_mid, b_mid, w_logits, b_logits):
    features = single.astype(jnp.float32)
    average = jnp.mean(features, axis=-1, keepdims=True)
    centred = features - average
    variance = jnp.mean(centred * centred, axis=-1, keepdims=True)
    normed = (centred * lax.rsqrt(variance + 1e-05) * ln_gain).astype(jnp.bfloat16)
    first_hidden = jax.nn.relu(
        jnp.dot(normed, w_hidden, preferred_element_type=jnp.float32) + b_hidden
    ).astype(jnp.bfloat16)
    second_hidden = jax.nn.relu(
        jnp.dot(first_hidden, w_mid, preferred_element_type=jnp.float32) + b_mid
    ).astype(jnp.bfloat16)
    logits = jnp.dot(second_hidden, w_logits, preferred_element_type=jnp.float32) + b_logits
    log_total = jnp.log(jnp.sum(jnp.exp(logits), axis=-1))
    bins = logits.shape[-1]
    centers = (jnp.arange(bins).astype(jnp.float32) + 0.5) / bins
    closeness = jnp.exp(-((lddt_value[..., None] - centers) ** 2) * (bins * bins * 0.5))
    target = closeness / jnp.sum(closeness, axis=-1, keepdims=True)
    return log_total - jnp.sum(target * logits, axis=-1)


def local(
    neighbor,
    true_coords,
    pred_coords,
    residue_mask,
    single,
    ln_gain,
    w_hidden,
    b_hidden,
    w_mid,
    b_mid,
    w_logits,
    b_logits,
):
    valid = residue_mask.astype(jnp.float32)
    stacked = jnp.concatenate([true_coords, pred_coords, valid[:, None, :]], axis=1)
    row_count = lax.axis_size("row")
    col_count = lax.axis_size(COL)
    rows_len = L // row_count
    cols_len = L // col_count
    col_index = lax.axis_index(COL)
    rows_part = gather_directly(stacked, COL, 2)
    offset = col_index * cols_len % rows_len
    column_piece = lax.dynamic_slice_in_dim(rows_part, offset, cols_len, 2)
    source_row = col_index * cols_len // rows_len
    cols_part = from_root(column_piece, "row", source_row)
    true_dist = tile_dist(rows_part[:, 0:3], cols_part[:, 0:3])
    pred_dist = tile_dist(rows_part[:, 3:6], cols_part[:, 3:6])
    mismatch = jnp.abs(pred_dist - true_dist)
    scores = jnp.zeros_like(mismatch)
    for threshold in THRESHOLDS:
        scores = scores + jax.nn.sigmoid(4.0 * (threshold - mismatch))
    scores = 0.25 * scores
    weights = neighbor.astype(jnp.float32) * rows_part[:, 6, None, :] * cols_part[:, 6, :, None]
    preserved = jnp.sum(weights * scores, axis=1)
    neighbors = jnp.sum(weights, axis=1)
    preserved_own, neighbors_own = sent_together((preserved, neighbors), COL, 1, 0)
    lddt_score = preserved_own / jnp.maximum(neighbors_own, 1.0)
    residue_loss = valid * head_loss(
        lddt_score, single, ln_gain, w_hidden, b_hidden, w_mid, b_mid, w_logits, b_logits
    )
    loss_sum, valid_sum = (
        over_axes(jnp.sum(residue_loss), ROW_COL),
        over_axes(jnp.sum(valid), ROW_COL),
    )
    total_loss = loss_sum / valid_sum
    return (lddt_score, residue_loss, total_loss)


def solution(mesh):
    torus = Mesh(
        mesh.devices.reshape(mesh.shape["row"], 4, 4, 2), ("row", "col_0", "col_1", "col_2")
    )
    placed = (
        P(None, COL, "row"),
        P(None, None, ROW_COL),
        P(None, None, ROW_COL),
        P(None, ROW_COL),
        P(None, ROW_COL, None),
        P(),
        P(),
        P(),
        P(),
        P(),
        P(),
        P(),
    )
    return jax.shard_map(
        local,
        mesh=torus,
        in_specs=placed,
        out_specs=(P(None, ROW_COL), P(None, ROW_COL), P()),
        check_vma=False,
    )
```

profile of v0, /device:TPU:1, one launch (start us, length us, event | category | flops | bytes accessed | tf_op | source)
XLA Modules:
  0.0 134.1 jit_solution(17454920612350802530)
XLA Ops:
  0.6 0.0 copy-start
  0.6 0.8 copy.19
  1.5 0.1 copy.20
  1.5 0.8 pad_maximum_fusion.1
  2.3 0.2 broadcast_bitcast_fusion
  2.5 2.1 %reshape.49 = f32[32,1,5376]{2,1,0:T(1,128)} reshape(f32[32,7,24,32]{3,2,1,0:T(8,128)S(1)} %broadcast_bitcast_fusion) | data formatting | bytes 1376256
  4.6 8.6 %all-to-all-start = ((f32[32,1,5376]{2,1,0:T(1,128)}), f32[32,1,5376]{2,1,0:T(1,128)S(1)}, u32[]{:S(2)}, u32[]{:S(2)}) async-start(f32[32,1,5376]{2,1,0:T(1,128)} %reshape.49), calls=%async_computation | async-start | bytes 1376256 | tf_op jit(solution)/shard_map/all_to_all | solution.py:21
  13.2 1.2 convert_reduce_fusion
  14.4 0.5 add_multiply_fusion
  15.0 1.4 %fusion.8 = f32[32,24]{1,0:T(8,128)S(1)} fusion(bf16[32,24,384]{2,1,0:T(8,128)(2,1)} %param.16, f32[32,24]{1,0:T(8,128)S(1)} %broadcast_multiply_fusion), kind=kLoop, calls=%fused_computation.15 | loop fusion | flops 1178880 | bytes 595968 | tf_op jit(solution)/shard_map/reduce_sum | solution.py:69
  16.4 0.0 copy-done
  16.4 2.6 %fusion.12 = bf16[32,24,128]{2,1,0:T(8,128)(2,1)} fusion(bf16[32,24,384]{2,1,0:T(8,128)(2,1)} %param.16, f32[384]{0:T(512)} %param.17, f32[32,24]{1,0:T(8,128)S(1)} %add_rsqrt_fusion, f32[32,24]{1,0:T(8,128)S(1)} %broadcast_multiply_fusion, f32[128]{0:T(128)} %param.21, f32[128]{0:T(128)} %param.19, bf16[384,128]{1,0:T(8,128)(2,1)S(1)} %copy-done, ...), kind=kOutput, calls=%fused_computation.19 | convolution fusion | flops 102727680 | bytes 926208 | tf_op jit(solution)/shard_map/dot_general | solution.py:75
  19.0 7.5 %all-to-all-done = f32[32,1,5376]{2,1,0:T(1,128)S(1)} async-done(((f32[32,1,5376]{2,1,0:T(1,128)}), f32[32,1,5376]{2,1,0:T(1,128)S(1)}, u32[]{:S(2)}, u32[]{:S(2)}) %all-to-all-start) | async-done | bytes 688160 | tf_op jit(solution)/shard_map/all_to_all | solution.py:21
  26.4 0.5 broadcast.53
  26.9 2.3 %reduce = f32[32,5376]{1,0:T(8,128)S(1)} reduce(f32[32,1,5376]{2,1,0:T(1,128)S(1)} %all-to-all-done, f32[]{:T(128)} %broadcast.53), dimensions={1}, to_apply=%all_to_all.6.reduce_sub_computation | reduce | bytes 1376260 | tf_op jit(solution)/shard_map/all_to_all | solution.py:21
  29.2 0.8 reshape.50
  30.0 1.7 %bitcast_bitcast_fusion = f32[32,7,32,24]{0,3,1,2:T(8,128)} fusion(f32[32,7,24,32]{3,2,1,0:T(8,128)S(1)} %reshape.50), kind=kLoop, calls=%fused_computation.64 | loop fusion | bytes 1376256 | tf_op jit(solution)/shard_map/transpose | solution.py:14
  31.7 5.6 %copy.21 = f32[32,7,32,24]{3,2,0,1:T(8,128)} copy(f32[32,7,32,24]{0,3,1,2:T(8,128)} %bitcast_bitcast_fusion) | data formatting | bytes 1376256 | tf_op jit(solution)/shard_map/transpose | solution.py:14
  37.3 3.6 %reshape.43 = f32[32,7,768]{2,0,1:T(8,128)S(1)} reshape(f32[32,7,32,24]{3,2,0,1:T(8,128)} %copy.21) | data formatting | bytes 1376256 | tf_op jit(solution)/shard_map/reshape | solution.py:16
  40.9 0.1 constant_dynamic-slice_fusion
  41.0 12.0 %all-gather = f32[128,7,96]{2,0,1:T(8,128)S(1)} all-gather(f32[32,7,96]{2,0,1:T(8,128)S(1)} %constant_dynamic-slice_fusion), channel_id=2, replica_groups=mesh['row'=4,'col_0'=4,'col_1'=4,'col_2'=2] {'row'}, dimensions={0}, use_global_device_ids=true | all-gather | bytes 430080 | tf_op jit(solution)/shard_map/all_gather | solution.py:29
  53.1 0.0 copy-start.1
  53.1 0.0 copy-start.3
  53.1 0.0 copy-start.4
  53.1 0.0 copy-start.5
  53.1 26.3 %multiply_reduce_fusion = (f32[32,768]{1,0:T(8,128)S(1)}, f32[32,768]{1,0:T(8,128)S(1)}) fusion(s32[32,96,768]{2,1,0:T(8,128)} %param.12, f32[32,768]{1,0:T(8,128)S(1)} %get-tuple-element.19, f32[32,96]{1,0:T(8,128)S(1)} %get-tuple-element.26, f32[32,768]{1,0:T(8,128)S(1)} %get-tuple-element.20, f32[32,96]{1,0:T(8,128)S(1)} %get-tuple-element.27, ...), kind=kLoop, calls=%fused_computation.1 | loop fusion | flops 117915648 | bytes 10407936 | tf_op jit(solution)/shard_map/reduce_sum | solution.py:120
  79.5 0.2 copy.22
  79.6 0.9 reshape.51
  80.6 5.6 %all-to-all-start.1 = ((f32[32,1,1536]{2,1,0:T(1,128)}), f32[32,1,1536]{2,1,0:T(1,128)S(1)}, u32[]{:S(2)}, u32[]{:S(2)}) async-start(f32[32,1,1536]{2,1,0:T(1,128)} %reshape.51), calls=%async_computation.1 | async-start | bytes 393216 | tf_op jit(solution)/shard_map/all_to_all | solution.py:39
  86.1 0.0 copy-done.1
  86.1 0.0 copy-done.3
  86.2 0.0 copy-done.4
  86.2 0.3 exponential_reduce_fusion
  86.5 8.0 %all-to-all-done.1 = f32[32,1,1536]{2,1,0:T(1,128)S(1)} async-done(((f32[32,1,1536]{2,1,0:T(1,128)}), f32[32,1,1536]{2,1,0:T(1,128)S(1)}, u32[]{:S(2)}, u32[]{:S(2)}) %all-to-all-start.1) | async-done | bytes 196640 | tf_op jit(solution)/shard_map/all_to_all | solution.py:39
  94.5 1.1 reduce.1
  95.6 0.1 reshape.52
  95.8 0.1 fusion.31
  95.8 0.0 copy-start.2
  95.9 0.1 copy.23
  95.9 0.0 copy-done.5
  95.9 0.6 fusion.35
  96.6 0.6 fusion.34
  97.2 0.7 copy.24
  97.8 9.7 %all-reduce.2 = (f32[]{:T(128)}, f32[]{:T(128)}) all-reduce(f32[]{:T(128)} %get-tuple-element.16, f32[]{:T(128)} %get-tuple-element.32), channel_id=1, replica_groups=mesh['row'=4,'col_0'=4,'col_1'=4,'col_2'=2] {'row'}, use_global_device_ids=true, to_apply=%region_9.10 | all-reduce | flops 2 | bytes 16 | tf_op jit(solution)/shard_map/psum | solution.py:54
  107.6 7.4 %all-reduce.1 = (f32[]{:T(128)}, f32[]{:T(128)}) all-reduce(f32[]{:T(128)} %get-tuple-element.12, f32[]{:T(128)} %get-tuple-element.13), channel_id=1, replica_groups=mesh['row'=4,'col_0'=4,'col_1'=4,'col_2'=2] {'col_0'}, use_global_device_ids=true, to_apply=%region_10.11 | all-reduce | flops 2 | bytes 16 | tf_op jit(solution)/shard_map/psum | solution.py:54
  115.0 7.7 %all-reduce = (f32[]{:T(128)}, f32[]{:T(128)}) all-reduce(f32[]{:T(128)} %get-tuple-element.10, f32[]{:T(128)} %get-tuple-element.11), channel_id=1, replica_groups=mesh['row'=4,'col_0'=4,'col_1'=4,'col_2'=2] {'col_1'}, use_global_device_ids=true, to_apply=%region_11.12 | all-reduce | flops 2 | bytes 16 | tf_op jit(solution)/shard_map/psum | solution.py:54
  122.7 9.1 %all-reduce.3 = (f32[]{:T(128)}, f32[]{:T(128)}) all-reduce(f32[]{:T(128)} %get-tuple-element.8, f32[]{:T(128)} %get-tuple-element.9), channel_id=1, replica_groups=mesh['row'=4,'col_0'=4,'col_1'=4,'col_2'=2] {'col_2'}, use_global_device_ids=true, to_apply=%region_12.13 | all-reduce | flops 2 | bytes 16 | tf_op jit(solution)/shard_map/psum | solution.py:54
  133.0 0.0 copy-done.2
  (8 shorter events, 0.1 us)
Async XLA Ops:
  0.6 15.7 %copy-start = (bf16[384,128]{1,0:T(8,128)(2,1)S(1)}, bf16[384,128]{1,0:T(8,128)(2,1)}, u32[]{:S(2)}) copy-start(bf16[384,128]{1,0:T(8,128)(2,1)} %param.18) | copy-start | bytes 294916
  4.6 21.8 %all-to-all-start = ((f32[32,1,5376]{2,1,0:T(1,128)}), f32[32,1,5376]{2,1,0:T(1,128)S(1)}, u32[]{:S(2)}, u32[]{:S(2)}) async-start(f32[32,1,5376]{2,1,0:T(1,128)} %reshape.49), calls=%async_computation | async-start | bytes 1376256 | tf_op jit(solution)/shard_map/all_to_all | solution.py:21
  53.1 33.1 %copy-start.1 = (bf16[32,24,128]{2,1,0:T(8,128)(2,1)S(1)}, bf16[32,24,128]{2,1,0:T(8,128)(2,1)}, u32[]{:S(2)}) copy-start(bf16[32,24,128]{2,1,0:T(8,128)(2,1)} %fusion.12) | copy-start | bytes 589828
  53.1 33.1 %copy-start.3 = (bf16[128,50]{0,1:T(8,128)(2,1)S(1)}, bf16[128,50]{0,1:T(8,128)(2,1)}, u32[]{:S(2)}) copy-start(bf16[128,50]{0,1:T(8,128)(2,1)} %param.22) | copy-start | bytes 38404
  53.1 33.1 %copy-start.4 = (f32[50]{0:T(128)S(1)}, f32[50]{0:T(128)}, u32[]{:S(2)}) copy-start(f32[50]{0:T(128)} %param.23) | copy-start | bytes 604
  53.1 42.8 %copy-start.5 = (f32[50]{0:T(128)S(1)}, f32[50]{0:T(128)}, u32[]{:S(2)}) copy-start(f32[50]{0:T(128)} %add_multiply_fusion) | copy-start | bytes 604
  80.6 13.9 %all-to-all-start.1 = ((f32[32,1,1536]{2,1,0:T(1,128)}), f32[32,1,1536]{2,1,0:T(1,128)S(1)}, u32[]{:S(2)}, u32[]{:S(2)}) async-start(f32[32,1,1536]{2,1,0:T(1,128)} %reshape.51), calls=%async_computation.1 | async-start | bytes 393216 | tf_op jit(solution)/shard_map/all_to_all | solution.py:39
  95.8 37.2 %copy-start.2 = (f32[32,24]{0,1:T(8,128)}, f32[32,24]{0,1:T(8,128)S(1)}, u32[]{:S(2)}) copy-start(f32[32,24]{0,1:T(8,128)S(1)} %fusion.31) | copy-start | bytes 9220
where the time goes:
time: 135 us; the launch traced here: 134 us
  blocking collectives  45.9 us (34%)
  other arithmetic  35 us (26%)
  local copies, waits for them, and re-layouts  17.4 us (13%)
  waiting for transfers between devices  15.4 us (11%)
  starting transfers between devices  14.2 us (11%)
  between operations  3.24 us (2%)
  matrix products  2.91 us (2%)
    psum x4, blocking collectives, over_axes(): shard = lax.psum(shard, axis)  33.9 us
    reduce_sum x1, other arithmetic, local(): preserved = jnp.sum(weights * scores, axis=1)  26.3 us
    all_gather x1, blocking collectives, from_root(): lax.all_gather(shard, axis)  12 us
    all_to_all x1, starting transfers between devices, sent_to_all(): return lax.all_to_all(copies, axis, split_axis=0, concat_axis=0, tiled=True)  8.58 us
    all_to_all x1, waiting for transfers between devices, summed_on_arrival(): parts = lax.all_to_all(split_up(shard, dim, size), axis, 0, 0, tiled=True)  7.99 us
    all_to_all x1, waiting for transfers between devices, sent_to_all(): return lax.all_to_all(copies, axis, split_axis=0, concat_axis=0, tiled=True)  7.45 us
    transpose x2, local copies, waits for them, and re-layouts, in_order(): parts = jnp.moveaxis(parts, 0, dim)  7.29 us
    unnamed x19, local copies, waits for them, and re-layouts  5.59 us
  transfers between devices with their start and end apart: 2, of which 2 were waited for; matrix products, arithmetic and copies ran while one was open for 5% of the time, Pallas kernels for 0%

commit v1 on v0

--- a/solution.py
+++ b/solution.py
@@ -51,7 +51,7 @@
 
 def over_axes(shard, axes):
     for axis in axes:
-        shard = lax.psum(shard, axis)
+        shard = jnp.sum(lax.all_gather(shard, axis), axis=0)
     return shard
 
 

time: 135 us -> 151 us (1.12)
  local copies, waits for them, and re-layouts: 17.4 us -> 31.8 us
  other arithmetic: 35 us -> 40.2 us
  blocking collectives: 45.9 us -> 43.2 us
    psum x4 -> x0, blocking collectives: 33.9 us -> none  [over_axes(): shard = lax.psum(shard, axis)]
    unnamed x0 -> x4, blocking collectives: none -> 31.2 us
    unnamed x19 -> x45, local copies, waits for them, and re-layouts: 5.59 us -> 19.9 us
    reduce_sum x0 -> x8, other arithmetic: none -> 5.13 us  [over_axes(): shard = jnp.sum(lax.all_gather(shard, axis), axis=0)]
where the time goes in v1:
time: 151 us; the launch traced here: 150 us
  blocking collectives  43.2 us (29%)
  other arithmetic  40.2 us (27%)
  local copies, waits for them, and re-layouts  31.8 us (21%)
  starting transfers between devices  14.2 us (9%)
  waiting for transfers between devices  14.2 us (9%)
  between operations  3.41 us (2%)
  matrix products  2.91 us (2%)
    unnamed x4, blocking collectives  31.2 us
    reduce_sum x1, other arithmetic, local(): preserved = jnp.sum(weights * scores, axis=1)  26.3 us
    unnamed x45, local copies, waits for them, and re-layouts  19.9 us
    all_gather x1, blocking collectives, from_root(): lax.all_gather(shard, axis)  12 us
    all_to_all x1, starting transfers between devices, sent_to_all(): return lax.all_to_all(copies, axis, split_axis=0, concat_axis=0, tiled=True)  8.58 us
    all_to_all x1, waiting for transfers between devices, summed_on_arrival(): parts = lax.all_to_all(split_up(shard, dim, size), axis, 0, 0, tiled=True)  7.98 us
    transpose x2, local copies, waits for them, and re-layouts, in_order(): parts = jnp.moveaxis(parts, 0, dim)  7.29 us
    all_to_all x1, waiting for transfers between devices, sent_to_all(): return lax.all_to_all(copies, axis, split_axis=0, concat_axis=0, tiled=True)  6.2 us
  transfers between devices with their start and end apart: 2, of which 2 were waited for; matrix products, arithmetic and copies ran while one was open for 5% of the time, Pallas kernels for 0%

profile of v1, /device:TPU:1, one launch (start us, length us, event | category | flops | bytes accessed | tf_op | source)
XLA Modules:
  0.0 149.8 jit_solution(4222566395221166053)
XLA Ops:
  0.6 0.8 copy.19
  1.5 0.8 pad_maximum_fusion.1
  2.5 2.1 %reshape.89 = f32[32,1,5376]{2,1,0:T(1,128)} reshape(f32[32,7,24,32]{3,2,1,0:T(8,128)S(1)} %broadcast_bitcast_fusion) | data formatting | bytes 1376256
  4.6 8.6 %all-to-all-start = ((f32[32,1,5376]{2,1,0:T(1,128)}), f32[32,1,5376]{2,1,0:T(1,128)S(1)}, u32[]{:S(2)}, u32[]{:S(2)}) async-start(f32[32,1,5376]{2,1,0:T(1,128)} %reshape.89), calls=%async_computation | async-start | bytes 1376256 | tf_op jit(solution)/shard_map/all_to_all | solution.py:21
  13.2 1.2 convert_reduce_fusion
  14.4 0.5 add_multiply_fusion
  15.0 1.2 dynamic-slice
  16.2 1.4 fusion.8
  17.6 2.6 %fusion.12 = bf16[32,24,128]{2,1,0:T(8,128)(2,1)} fusion(bf16[32,24,384]{2,1,0:T(8,128)(2,1)} %param.16, f32[384]{0:T(512)} %param.17, f32[32,24]{1,0:T(8,128)S(1)} %add_rsqrt_fusion, f32[32,24]{1,0:T(8,128)S(1)} %broadcast_multiply_fusion, f32[128]{0:T(128)} %param.21, f32[128]{0:T(128)} %param.19, bf16[384,128]{1,0:T(8,128)(2,1)S(1)} %copy-done, ...), kind=kOutput, calls=%fused_computation.19 | convolution fusion | flops 102727680 | bytes 926208 | tf_op jit(solution)/shard_map/dot_general | solution.py:75
  20.2 6.2 %all-to-all-done = f32[32,1,5376]{2,1,0:T(1,128)S(1)} async-done(((f32[32,1,5376]{2,1,0:T(1,128)}), f32[32,1,5376]{2,1,0:T(1,128)S(1)}, u32[]{:S(2)}, u32[]{:S(2)}) %all-to-all-start) | async-done | bytes 688160 | tf_op jit(solution)/shard_map/all_to_all | solution.py:21
  26.4 0.5 broadcast.61
  26.9 2.3 %reduce.8 = f32[32,5376]{1,0:T(8,128)S(1)} reduce(f32[32,1,5376]{2,1,0:T(1,128)S(1)} %all-to-all-done, f32[]{:T(128)} %broadcast.61), dimensions={1}, to_apply=%all_to_all.6.reduce_sub_computation | reduce | bytes 1376260 | tf_op jit(solution)/shard_map/all_to_all | solution.py:21
  29.2 0.8 reshape.90
  30.0 1.7 %bitcast_bitcast_fusion = f32[32,7,32,24]{0,3,1,2:T(8,128)} fusion(f32[32,7,24,32]{3,2,1,0:T(8,128)S(1)} %reshape.90), kind=kLoop, calls=%fused_computation.64 | loop fusion | bytes 1376256 | tf_op jit(solution)/shard_map/transpose | solution.py:14
  31.7 5.6 %copy.21 = f32[32,7,32,24]{3,2,0,1:T(8,128)} copy(f32[32,7,32,24]{0,3,1,2:T(8,128)} %bitcast_bitcast_fusion) | data formatting | bytes 1376256 | tf_op jit(solution)/shard_map/transpose | solution.py:14
  37.3 3.6 %reshape.43 = f32[32,7,768]{2,0,1:T(8,128)S(1)} reshape(f32[32,7,32,24]{3,2,0,1:T(8,128)} %copy.21) | data formatting | bytes 1376256 | tf_op jit(solution)/shard_map/reshape | solution.py:16
  41.0 12.0 %all-gather = f32[128,7,96]{2,0,1:T(8,128)S(1)} all-gather(f32[32,7,96]{2,0,1:T(8,128)S(1)} %constant_dynamic-slice_fusion), channel_id=2, replica_groups=mesh['row'=4,'col_0'=4,'col_1'=4,'col_2'=2] {'row'}, dimensions={0}, use_global_device_ids=true | all-gather | bytes 430080 | tf_op jit(solution)/shard_map/all_gather | solution.py:29
  53.2 26.3 %multiply_reduce_fusion = (f32[32,768]{1,0:T(8,128)S(1)}, f32[32,768]{1,0:T(8,128)S(1)}) fusion(s32[32,96,768]{2,1,0:T(8,128)} %param.12, f32[32,768]{1,0:T(8,128)S(1)} %get-tuple-element.19, f32[32,96]{1,0:T(8,128)S(1)} %get-tuple-element.26, f32[32,768]{1,0:T(8,128)S(1)} %get-tuple-element.20, f32[32,96]{1,0:T(8,128)S(1)} %get-tuple-element.27, ...), kind=kLoop, calls=%fused_computation.1 | loop fusion | flops 117915648 | bytes 10407936 | tf_op jit(solution)/shard_map/reduce_sum | solution.py:120
  79.7 0.9 reshape.91
  80.6 5.6 %all-to-all-start.1 = ((f32[32,1,1536]{2,1,0:T(1,128)}), f32[32,1,1536]{2,1,0:T(1,128)S(1)}, u32[]{:S(2)}, u32[]{:S(2)}) async-start(f32[32,1,1536]{2,1,0:T(1,128)} %reshape.91), calls=%async_computation.1 | async-start | bytes 393216 | tf_op jit(solution)/shard_map/all_to_all | solution.py:39
  86.6 8.0 %all-to-all-done.1 = f32[32,1,1536]{2,1,0:T(1,128)S(1)} async-done(((f32[32,1,1536]{2,1,0:T(1,128)}), f32[32,1,1536]{2,1,0:T(1,128)S(1)}, u32[]{:S(2)}, u32[]{:S(2)}) %all-to-all-start.1) | async-done | bytes 196640 | tf_op jit(solution)/shard_map/all_to_all | solution.py:39
  94.5 1.1 reduce.9
  96.0 0.6 fusion.35
  96.6 0.6 fusion.34
  97.2 1.4 dynamic-update-slice
  98.6 1.4 dynamic-update-slice.4
  100.0 0.6 dynamic-slice.1
  100.6 9.0 %all-reduce.10 = (f32[4]{0:T(128)S(1)}, f32[4]{0:T(128)S(1)}) all-reduce(f32[4]{0:T(128)S(1)} %dynamic-update-slice, f32[4]{0:T(128)S(1)} %dynamic-update-slice.4), channel_id=1, replica_groups=mesh['row'=4,'col_0'=4,'col_1'=4,'col_2'=2] {'row'}, use_global_device_ids=true, to_apply=%add | all-reduce | flops 8 | bytes 64
  109.6 0.6 reduce_sum.171
  110.2 0.7 reduce_sum.176
  110.9 1.4 dynamic-update-slice.1
  112.3 1.4 dynamic-update-slice.5
  113.7 0.6 dynamic-slice.2
  114.3 6.8 %all-reduce.9 = (f32[4]{0:T(128)S(1)}, f32[4]{0:T(128)S(1)}) all-reduce(f32[4]{0:T(128)S(1)} %dynamic-update-slice.1, f32[4]{0:T(128)S(1)} %dynamic-update-slice.5), channel_id=1, replica_groups=mesh['row'=4,'col_0'=4,'col_1'=4,'col_2'=2] {'col_0'}, use_global_device_ids=true, to_apply=%add.1 | all-reduce | flops 8 | bytes 64
  121.1 0.6 reduce_sum.172
  121.7 0.7 reduce_sum.177
  122.3 1.4 dynamic-update-slice.2
  123.8 1.4 dynamic-update-slice.6
  125.2 0.6 dynamic-slice.3
  125.8 7.0 %all-reduce.8 = (f32[4]{0:T(128)S(1)}, f32[4]{0:T(128)S(1)}) all-reduce(f32[4]{0:T(128)S(1)} %dynamic-update-slice.2, f32[4]{0:T(128)S(1)} %dynamic-update-slice.6), channel_id=1, replica_groups=mesh['row'=4,'col_0'=4,'col_1'=4,'col_2'=2] {'col_1'}, use_global_device_ids=true, to_apply=%add.2 | all-reduce | flops 8 | bytes 64
  132.8 0.6 reduce_sum.173
  133.4 0.7 reduce_sum.178
  134.1 1.4 dynamic-update-slice.3
  135.5 1.4 dynamic-update-slice.7
  136.9 0.7 copy.24
  137.6 8.5 %all-reduce.11 = (f32[2]{0:T(128)S(1)}, f32[2]{0:T(128)S(1)}) all-reduce(f32[2]{0:T(128)S(1)} %dynamic-update-slice.3, f32[2]{0:T(128)S(1)} %dynamic-update-slice.7), channel_id=1, replica_groups=mesh['row'=4,'col_0'=4,'col_1'=4,'col_2'=2] {'col_2'}, use_global_device_ids=true, to_apply=%add.3 | all-reduce | flops 4 | bytes 32
  146.0 0.6 reduce_sum.174
  146.6 0.7 reduce_sum.179
  (42 shorter events, 1.3 us)
Async XLA Ops:
  0.6 17.0 %copy-start = (bf16[384,128]{1,0:T(8,128)(2,1)S(1)}, bf16[384,128]{1,0:T(8,128)(2,1)}, u32[]{:S(2)}) copy-start(bf16[384,128]{1,0:T(8,128)(2,1)} %param.18) | copy-start | bytes 294916
  4.6 21.8 %all-to-all-start = ((f32[32,1,5376]{2,1,0:T(1,128)}), f32[32,1,5376]{2,1,0:T(1,128)S(1)}, u32[]{:S(2)}, u32[]{:S(2)}) async-start(f32[32,1,5376]{2,1,0:T(1,128)} %reshape.89), calls=%async_computation | async-start | bytes 1376256 | tf_op jit(solution)/shard_map/all_to_all | solution.py:21
  53.1 33.1 %copy-start.1 = (bf16[32,24,128]{2,1,0:T(8,128)(2,1)S(1)}, bf16[32,24,128]{2,1,0:T(8,128)(2,1)}, u32[]{:S(2)}) copy-start(bf16[32,24,128]{2,1,0:T(8,128)(2,1)} %fusion.12) | copy-start | bytes 589828
  53.1 33.1 %copy-start.3 = (bf16[128,50]{0,1:T(8,128)(2,1)S(1)}, bf16[128,50]{0,1:T(8,128)(2,1)}, u32[]{:S(2)}) copy-start(bf16[128,50]{0,1:T(8,128)(2,1)} %param.22) | copy-start | bytes 38404
  53.1 33.1 %copy-start.4 = (f32[50]{0:T(128)S(1)}, f32[50]{0:T(128)}, u32[]{:S(2)}) copy-start(f32[50]{0:T(128)} %param.23) | copy-start | bytes 604
  53.1 42.9 %copy-start.8 = (f32[50]{0:T(128)S(1)}, f32[50]{0:T(128)}, u32[]{:S(2)}) copy-start(f32[50]{0:T(128)} %add_multiply_fusion) | copy-start | bytes 604
  53.1 46.9 %copy-start.7 = (u32[128]{0:T(128)S(1)}, u32[128]{0:T(128)}, u32[]{:S(2)}) copy-start(u32[128]{0:T(128)} %constant.82) | copy-start | bytes 1540
  53.1 60.6 %copy-start.6 = (u32[128]{0:T(128)S(1)}, u32[128]{0:T(128)}, u32[]{:S(2)}) copy-start(u32[128]{0:T(128)} %constant.87) | copy-start | bytes 1540
  53.2 72.0 %copy-start.5 = (u32[128]{0:T(128)S(1)}, u32[128]{0:T(128)}, u32[]{:S(2)}) copy-start(u32[128]{0:T(128)} %constant.92) | copy-start | bytes 1540
  80.6 13.9 %all-to-all-start.1 = ((f32[32,1,1536]{2,1,0:T(1,128)}), f32[32,1,1536]{2,1,0:T(1,128)S(1)}, u32[]{:S(2)}, u32[]{:S(2)}) async-start(f32[32,1,1536]{2,1,0:T(1,128)} %reshape.91), calls=%async_computation.1 | async-start | bytes 393216 | tf_op jit(solution)/shard_map/all_to_all | solution.py:39
  95.9 52.8 %copy-start.2 = (f32[32,24]{0,1:T(8,128)}, f32[32,24]{0,1:T(8,128)S(1)}, u32[]{:S(2)}) copy-start(f32[32,24]{0,1:T(8,128)S(1)} %fusion.31) | copy-start | bytes 9220
